TPU v7x, 32 devices: a whole 2x2x4 slice. The times are simulated.
32 devices in a mesh: ep: 4 (over y, core), fsdp: 8 (over z, x).
Axes of the slice: x: 2, y: 2, z: 4, core: 2. Of those that a mesh axis runs over, the one named last changes fastest.
Arguments:
- w_down: float32 [16, 6400, 4096], P('ep', None, 'fsdp'), may hold values from -0.109375 to 0.109375
- router_weight: float32 [4096, 16], P('fsdp', 'ep'), may hold values from -0.09375 to 0.09375
- router_gain: float32 [4096], P('fsdp'), may hold values from 0.25 to 1.75
Outputs:
- serve_down: bfloat16 [16, 6400, 4096], P('ep', 'fsdp')
- scale_down: float32 [16, 6400], P('ep', 'fsdp')
- serve_router: bfloat16 [4096, 16], replicated
All inputs are finite; a program needn't handle non-finite values.
Results may differ from a plain program's by a relative error of at most 0.001.
Values may be sent and summed in bfloat16 or wider, within the bound.
A program may use at most 192 MiB of HBM per device.

v0:
```python
import jax
import jax.numpy as jnp
from jax import lax
from jax.sharding import PartitionSpec as P


def body(w_down, router_weight, router_gain):
    total_down = lax.psum(jnp.sum(w_down * w_down, axis=2), "fsdp")
    scale_down = jnp.sqrt(total_down)
    narrow_down = (w_down / jnp.expand_dims(scale_down, 2)).astype(jnp.bfloat16)
    serve_down = lax.all_to_all(narrow_down, "fsdp", split_axis=1, concat_axis=2, tiled=True)
    scale_down = lax.dynamic_slice_in_dim(
        scale_down, lax.axis_index("fsdp") * serve_down.shape[1], serve_down.shape[1], axis=1
    )
    part_router = (router_weight * router_gain[:, None]).astype(jnp.bfloat16)
    row_router = lax.all_gather(part_router, "fsdp", axis=0, tiled=True)
    serve_router = lax.all_gather(row_router, "ep", axis=1, tiled=True)
    return (serve_down, scale_down, serve_router)


def solution(mesh):
    in_specs = (P("ep", None, "fsdp"), P("fsdp", "ep"), P("fsdp"))
    out_specs = (P("ep", "fsdp", None), P("ep", "fsdp"), P())
    return jax.shard_map(body, mesh=mesh, in_specs=in_specs, out_specs=out_specs, check_vma=False)
```

profile of v0, /device:TPU:0, one launch (start us, length us, event | category | flops | bytes accessed | tf_op | source)
XLA Modules:
  0.0 818.4 jit_solution(10136285089813340323)
XLA Ops:
  7.2 0.0 all-reduce.2.cloned.1.call-start
  7.2 17.4 %multiply_reduce_fusion = f32[4,6400]{1,0:T(4,128)} fusion(f32[4,6400,512]{2,1,0:T(8,128)} %param.3), kind=kLoop, calls=%fused_computation.1 | loop fusion | flops 26188800 | bytes 52531200 | tf_op jit(solution)/shard_map/reduce_sum | solution.py:8
  24.6 0.0 all-reduce.2.cloned.1.call-update
  24.6 72.5 %all-reduce.2.cloned.1.call-done = f32[4,6400]{1,0:T(4,128)} async-done(((f32[4,6400]{1,0:T(4,128)}), f32[4,6400]{1,0:T(4,128)}) %all-reduce.2.cloned.1.call-update) | async-done | bytes 102416 | tf_op jit(solution)/shard_map/psum | solution.py:8
  97.1 0.9 sqrt.3
  98.1 1.1 copy.7
  99.2 0.0 copy-start
  99.2 0.0 copy-start.1
  99.2 58.2 %fusion = bf16[4,6400,512]{2,0,1:T(4,128)(2,1)} fusion(f32[4,6400,512]{2,1,0:T(8,128)} %param.3, f32[4,6400]{0,1:T(8,128)S(1)} %copy.7), kind=kLoop, calls=%fused_computation.2 | loop fusion | flops 26214400 | bytes 78745600 | tf_op jit(solution)/shard_map/convert_element_type | solution.py:10
  157.4 6.5 all-to-all-start
  163.9 0.0 copy-done
  163.9 0.0 copy-done.1
  163.9 583.4 %all_gather.6 = bf16[4096,4]{0,1:T(4,128)(2,1)S(1)} all-gather(bf16[512,4]{0,1:T(4,128)(2,1)S(1)} %multiply_convert_fusion), channel_id=1, replica_groups=mesh['ep'=4,'fsdp'=8] {'fsdp'}, dimensions={0}, use_global_device_ids=true | all-gather | bytes 36864 | tf_op jit(solution)/shard_map/all_gather | solution.py:16
  747.3 5.4 all-gather
  752.8 0.7 reshape.9
  753.4 0.7 constant_dynamic-slice_fusion
  754.1 0.0 all-to-all-done
  754.1 18.2 %copy.9 = bf16[4,800,8,512]{3,2,1,0:T(8,128)(2,1)} copy(bf16[4,800,8,512]{3,0,1,2:T(4,128)(2,1)} %bitcast.1) | data formatting | bytes 52428800 | tf_op jit(solution)/shard_map/all_to_all | solution.py:11
  772.3 39.2 %all_to_all.16 = bf16[4,800,4096]{2,1,0:T(8,128)(2,1)} reshape(bf16[4,800,8,512]{3,2,1,0:T(8,128)(2,1)} %copy.9) | data formatting | bytes 52428800 | tf_op jit(solution)/shard_map/all_to_all | solution.py:11
  (1 shorter events, 0.0 us)
Async XLA Ops:
  7.2 90.0 %all-reduce.2.cloned.1.call-start = ((), (), s32[]{:S(2)}) async-start(), calls=%async_computation.1 | async-start | bytes 204800 | tf_op jit(solution)/shard_map/psum | solution.py:8
  99.2 64.7 %copy-start = (f32[512,4]{0,1:T(4,128)S(1)}, f32[512,4]{0,1:T(4,128)}, u32[]{:S(2)}) copy-start(f32[512,4]{0,1:T(4,128)} %param.4) | copy-start | bytes 24580
  99.2 64.7 %copy-start.1 = (f32[512]{0:T(512)S(1)}, f32[512]{0:T(512)}, u32[]{:S(2)}) copy-start(f32[512]{0:T(512)} %param.5) | copy-start | bytes 6148
  157.4 596.7 %all-to-all-start = ((bf16[4,6400,512]{2,0,1:T(4,128)(2,1)}), bf16[4,6400,512]{2,0,1:T(4,128)(2,1)}, u32[]{:S(2)}, u32[]{:S(2)}) async-start(bf16[4,6400,512]{2,0,1:T(4,128)(2,1)} %fusion), calls=%async_computation | async-start | bytes 52428800 | tf_op jit(solution)/shard_map/all_to_all | solution.py:11
Sparse Core Ops, SparseCore 0:
  24.8 72.3 all-reduce.1
where the time goes:
time: 820 us; the launch traced here: 818 us
  blocking collectives  589 us (72%)
  other arithmetic  75.6 us (9%)
  waiting for transfers between devices  72.5 us (9%)
  local copies, waits for them, and re-layouts  60.8 us (7%)
  between operations  14.1 us (2%)
    all_gather x1, blocking collectives, body(): row_router = lax.all_gather(part_router, 'fsdp', axis=0, tiled=True)  583 us
    psum x1, waiting for transfers between devices, body(): total_down = lax.psum(jnp.sum(w_down * w_down, axis=2), 'fsdp')  72.5 us
    convert_element_type x1, other arithmetic, body(): narrow_down = (w_down / jnp.expand_dims(scale_down, 2)).astype(jnp.bfloat16)  58.2 us
    all_to_all x2, local copies, waits for them, and re-layouts, body(): lax.all_to_all(narrow_down, 'fsdp', split_axis=1, concat_axis=2, tiled=True)  57.4 us
    reduce_sum x1, other arithmetic, body(): total_down = lax.psum(jnp.sum(w_down * w_down, axis=2), 'fsdp')  17.4 us
  transfers between devices with their start and end apart: 2, of which 1 were waited for; matrix products, arithmetic and copies ran while one was open for 0% of the time, Pallas kernels for 0%

commit v1 on v0

v1 whole, which is shorter than its diff:
```python
import functools

import jax
import jax.numpy as jnp
from jax import lax
from jax.experimental import pallas as pl
from jax.experimental.pallas import tpu as pltpu
from jax.sharding import PartitionSpec as P

LANES = 128
MESH = pl.DeviceIdType.MESH


def target(me, j, n):
    h = n // 2
    side = me // h
    m = me + side * (n - 1 - 2 * me)
    inner = m // max(n // 4, 1)
    half = j // 2
    odd = j % 2
    d_in = (1 - odd) * (h + (half + m) % h) + odd * ((m + 1 + half) % h)
    far = (j + 1) // h
    d_out = (1 - far) * ((m + 1 + j) % h) + far * (h + (j + 1 - h + m) % h)
    d = inner * d_in + (1 - inner) * d_out
    d = d + side * (n - 1 - 2 * d)
    last = (j + 1) // n
    return last * me + (1 - last) * d


def kernel(n, w, o, sc, xbuf, sbuf, part, recvp, mine, scales,
           load_sem, send_sem, recv_sem, psend, precv, ssend, srecv, own_sem):
    experts, rows, cols = w.shape
    block = rows // n
    tiles = -(-block // LANES)
    padded = part.shape[2]
    starts = [min(t * LANES, block - LANES) for t in range(tiles)]
    steps = n * experts
    slots = xbuf.shape[0]
    me = lax.axis_index("fsdp")

    def where(i):
        return target(me, i // experts, n), i % experts

    def load(i):
        d, e = where(i)
        s = i % slots
        return pltpu.make_async_copy(
            w.at[e, pl.ds(pl.multiple_of(d * block, 8), block), :], xbuf.at[s], load_sem.at[s])

    def peer(j):
        return target(me, j, n)

    def sums(to, source):
        return pltpu.make_async_remote_copy(
            src_ref=part.at[to], dst_ref=recvp.at[source], send_sem=psend.at[to],
            recv_sem=precv.at[source], device_id={"fsdp": to}, device_id_type=MESH)

    def scale_copy(to, source):
        return pltpu.make_async_remote_copy(
            src_ref=mine, dst_ref=scales.at[source], send_sem=ssend.at[to],
            recv_sem=srecv.at[source], device_id={"fsdp": to}, device_id_type=MESH)

    def bulk(i, to, e, source):
        return pltpu.make_async_remote_copy(
            src_ref=sbuf.at[i],
            dst_ref=o.at[e, :, pl.ds(pl.multiple_of(source * cols, LANES), cols)],
            send_sem=send_sem.at[i], recv_sem=recv_sem.at[source * experts + e],
            device_id={"fsdp": to}, device_id_type=MESH)

    def local(i, e):
        return pltpu.make_async_copy(
            sbuf.at[i], o.at[e, :, pl.ds(pl.multiple_of(me * cols, LANES), cols)], own_sem.at[e])

    def each(count, f):
        def step(i, c):
            f(i)
            return c
        lax.fori_loop(0, count, step, 0)

    each(slots, lambda k: load(steps - 1 - k).start())

    barrier = pltpu.get_barrier_semaphore()
    each(n - 1, lambda j: pl.semaphore_signal(
        barrier, inc=1, device_id={"fsdp": peer(j)}, device_id_type=MESH))
    pl.semaphore_wait(barrier, n - 1)

    def first(k):
        i = steps - 1 - k
        d, e = where(i)
        s = i % slots
        load(i).wait()
        found = []
        for start in starts:
            x = xbuf[s, start:start + LANES, :]
            y = x * x
            acc = y[:, :LANES]
            for c in range(LANES, cols, LANES):
                acc = acc + y[:, c:c + LANES]
            found.append(jnp.sum(acc.T, axis=0, keepdims=True))
        if padded > tiles:
            found.append(jnp.zeros((padded - tiles, LANES), jnp.float32))
        part[d, e] = jnp.concatenate(found, axis=0)

        @pl.when(i >= slots)
        def _():
            load(i - slots).start()

        @pl.when((e == 0) & (i // experts < n - 1))
        def _():
            sums(d, me).start()

    each(steps, first)

    def add(j, total):
        source = peer(j)
        sums(source, source).wait_recv()
        return total + recvp[source]

    total = lax.fori_loop(0, n - 1, add, part[me])
    scale = jnp.sqrt(total)
    sc[...] = scale
    mine[...] = scale
    scales[me] = scale
    each(n - 1, lambda j: scale_copy(peer(j), me).start())

    def second(i):
        d, e = where(i)
        s = i % slots

        @pl.when((e == 0) & (i // experts < n - 1))
        def _():
            scale_copy(d, d).wait_recv()

        @pl.when(i >= slots)
        def _():
            load(i).wait()

        inverse = 1.0 / scales[d, e]
        for t, start in enumerate(starts):
            factor = jnp.broadcast_to(inverse[t:t + 1, :], (LANES, LANES)).T
            for c in range(0, cols, LANES):
                x = xbuf[s, start:start + LANES, c:c + LANES]
                sbuf[i, start:start + LANES, c:c + LANES] = (x * factor).astype(jnp.bfloat16)

        @pl.when(i + slots < steps)
        def _():
            load(i + slots).start()

        @pl.when(i // experts < n - 1)
        def _():
            bulk(i, d, e, me).start()

        @pl.when(i // experts == n - 1)
        def _():
            local(i, e).start()

    each(steps, second)

    def drain(i):
        d, e = where(i)
        bulk(i, d, e, me).wait_send()
        bulk(i, d, e, d).wait_recv()

    def finish(j):
        sums(peer(j), me).wait_send()
        scale_copy(peer(j), me).wait_send()

    each(n - 1, finish)
    each(experts, lambda e: local(steps - experts + e, e).wait())
    each(steps - experts, drain)


def exchange(n, w):
    experts, rows, cols = w.shape
    block = rows // n
    tiles = -(-block // LANES)
    padded = -(-tiles // 8) * 8
    steps = n * experts
    slots = min(2 * n, steps)
    sums = (n, experts, padded, LANES)
    dma = pltpu.SemaphoreType.DMA
    o, sc = pl.pallas_call(
        functools.partial(kernel, n),
        out_shape=(
            jax.ShapeDtypeStruct((experts, block, n * cols), jnp.bfloat16),
            jax.ShapeDtypeStruct((experts, padded, LANES), jnp.float32),
        ),
        in_specs=[pl.BlockSpec(memory_space=pl.ANY)],
        out_specs=(pl.BlockSpec(memory_space=pl.ANY), pl.BlockSpec(memory_space=pltpu.VMEM)),
        scratch_shapes=[
            pltpu.VMEM((slots, block, cols), jnp.float32),
            pltpu.VMEM((steps, block, cols), jnp.bfloat16),
            pltpu.VMEM(sums, jnp.float32),
            pltpu.VMEM(sums, jnp.float32),
            pltpu.VMEM(sums[1:], jnp.float32),
            pltpu.VMEM(sums, jnp.float32),
            dma((slots,)), dma((steps,)), dma((steps,)),
            dma((n,)), dma((n,)), dma((n,)), dma((n,)), dma((experts,)),
        ],
        compiler_params=pltpu.CompilerParams(
            collective_id=0, has_side_effects=True, vmem_limit_bytes=58 * 1024 * 1024),
    )(w)
    tail = block - (tiles - 1) * LANES
    scale = jnp.concatenate(
        [sc[:, :tiles - 1].reshape(experts, (tiles - 1) * LANES), sc[:, tiles - 1, LANES - tail:]], axis=1)
    return o, scale


def body(n, w_down, router_weight, router_gain):
    serve_down, scale_down = exchange(n, w_down)
    part_router = (router_weight * router_gain[:, None]).astype(jnp.bfloat16)
    row_router = lax.all_gather(part_router, "fsdp", axis=0, tiled=True)
    serve_router = lax.all_gather(row_router, "ep", axis=1, tiled=True)
    return (serve_down, scale_down, serve_router)


def solution(mesh):
    in_specs = (P("ep", None, "fsdp"), P("fsdp", "ep"), P("fsdp"))
    out_specs = (P("ep", "fsdp", None), P("ep", "fsdp"), P())
    return jax.shard_map(
        functools.partial(body, mesh.shape["fsdp"]), mesh=mesh,
        in_specs=in_specs, out_specs=out_specs, check_vma=False)
```

time: 820 us -> 680 us (0.83)
  Pallas kernels: 0 us -> 487 us
  blocking collectives: 589 us -> 172 us
  other arithmetic: 75.6 us -> 0.61 us
  waiting for transfers between devices: 72.5 us -> 0 us
  local copies, waits for them, and re-layouts: 60.8 us -> 20.1 us
  between operations: 14.1 us -> 0.66 us
    pallas_call x0 -> x1, Pallas kernels: none -> 487 us  [exchange(): pl.pallas_call(functools.partial(kernel, n), out_shape=(jax.ShapeDtypeStr...]
    all_gather x1, blocking collectives: 583 us -> 166 us  [body(): row_router = lax.all_gather(part_router, 'fsdp', axis=0, tiled=True)]
    psum x1 -> x0, waiting for transfers between devices: 72.5 us -> none  [body(): total_down = lax.psum(jnp.sum(w_down * w_down, axis=2), 'fsdp')]
    convert_element_type x1 -> x0, other arithmetic: 58.2 us -> none  [body(): narrow_down = (w_down / jnp.expand_dims(scale_down, 2)).astype(jnp.bfloat16)]
    all_to_all x2 -> x0, local copies, waits for them, and re-layouts: 57.4 us -> none  [body(): lax.all_to_all(narrow_down, 'fsdp', split_axis=1, concat_axis=2, tiled=True)]
    unnamed x5 -> x8, local copies, waits for them, and re-layouts: 0.7 us -> 19.4 us
    reduce_sum x1 -> x0, other arithmetic: 17.4 us -> none  [body(): total_down = lax.psum(jnp.sum(w_down * w_down, axis=2), 'fsdp')]
  transfers between devices with their start and end apart: 2 -> 0, of which waited for: 1 -> 0; matrix products, arithmetic and copies ran while one was open for 0% -> 0% of each run, Pallas kernels for 0% -> 0%
where the time goes in v1:
time: 680 us
  Pallas kernels  487 us (72%)
  blocking collectives  172 us (25%)
  local copies, waits for them, and re-layouts  20.1 us (3%)
    pallas_call x1, Pallas kernels, exchange(): pl.pallas_call(functools.partial(kernel, n), out_shape=(jax.ShapeDtypeStr...  487 us
    all_gather x1, blocking collectives, body(): row_router = lax.all_gather(part_router, 'fsdp', axis=0, tiled=True)  166 us
    unnamed x8, local copies, waits for them, and re-layouts  19.4 us

profile of v1, /device:TPU:0, one launch (start us, length us, event | category | flops | bytes accessed | tf_op | source)
XLA Modules:
  0.0 680.1 jit_solution(10910179753488263933)
XLA Ops:
  0.6 0.0 copy-start
  0.6 0.0 copy-start.1
  0.7 487.0 %shard_map.58 = (bf16[4,800,4096]{2,1,0:T(8,128)(2,1)}, f32[4,8,128]{2,1,0:T(8,128)}) custom-call(f32[4,6400,512]{2,1,0:T(8,128)} %w.1), custom_call_target="tpu_custom_call" | custom-call | tf_op jit(solution)/shard_map/pallas_call | solution.py:182
  487.6 0.7 slice_bitcast_fusion
  488.4 0.8 slice.7
  489.2 0.6 pad_maximum_fusion
  489.8 0.0 copy-done
  489.8 0.0 copy-done.1
  489.8 166.3 %all_gather.6 = bf16[4096,4]{0,1:T(4,128)(2,1)S(1)} all-gather(bf16[512,4]{0,1:T(4,128)(2,1)S(1)} %multiply_convert_fusion), channel_id=1, replica_groups=mesh['ep'=4,'fsdp'=8] {'fsdp'}, dimensions={0}, use_global_device_ids=true | all-gather | bytes 36864 | tf_op jit(solution)/shard_map/all_gather | solution.py:212
  656.1 5.4 all-gather
  661.5 0.7 reshape.12
  662.2 17.9 %copy.10 = bf16[4,800,4096]{2,1,0:T(8,128)(2,1)} copy(bf16[4,800,4096]{2,1,0:T(8,128)(2,1)} %get-tuple-element.10) | data formatting | bytes 52428800
  (2 shorter events, 0.0 us)
Async XLA Ops:
  0.6 489.1 %copy-start = (f32[512,4]{0,1:T(4,128)S(1)}, f32[512,4]{0,1:T(4,128)}, u32[]{:S(2)}) copy-start(f32[512,4]{0,1:T(4,128)} %param.4) | copy-start | bytes 24580
  0.6 489.1 %copy-start.1 = (f32[512]{0:T(512)S(1)}, f32[512]{0:T(512)}, u32[]{:S(2)}) copy-start(f32[512]{0:T(512)} %param.5) | copy-start | bytes 6148

commit v2 on v1

--- a/solution.py
+++ b/solution.py
@@ -12,19 +12,7 @@
 
 
 def target(me, j, n):
-    h = n // 2
-    side = me // h
-    m = me + side * (n - 1 - 2 * me)
-    inner = m // max(n // 4, 1)
-    half = j // 2
-    odd = j % 2
-    d_in = (1 - odd) * (h + (half + m) % h) + odd * ((m + 1 + half) % h)
-    far = (j + 1) // h
-    d_out = (1 - far) * ((m + 1 + j) % h) + far * (h + (j + 1 - h + m) % h)
-    d = inner * d_in + (1 - inner) * d_out
-    d = d + side * (n - 1 - 2 * d)
-    last = (j + 1) // n
-    return last * me + (1 - last) * d
+    return (me + j + 1) % n
 
 
 def kernel(n, w, o, sc, xbuf, sbuf, part, recvp, mine, scales,

time: 680 us -> 647 us (0.951)
  Pallas kernels: 487 us -> 449 us
    pallas_call x1, Pallas kernels: 487 us -> 449 us  [exchange(): pl.pallas_call(functools.partial(kernel, n), out_shape=(jax.ShapeDtypeStr...]
where the time goes in v2:
time: 647 us
  Pallas kernels  449 us (69%)
  blocking collectives  176 us (27%)
  local copies, waits for them, and re-layouts  20.1 us (3%)
    pallas_call x1, Pallas kernels, exchange(): pl.pallas_call(functools.partial(kernel, n), out_shape=(jax.ShapeDtypeStr...  449 us
    all_gather x1, blocking collectives, body(): row_router = lax.all_gather(part_router, 'fsdp', axis=0, tiled=True)  171 us
    unnamed x8, local copies, waits for them, and re-layouts  19.4 us

profile of v2, /device:TPU:0, one launch (start us, length us, event | category | flops | bytes accessed | tf_op | source)
XLA Modules:
  0.0 646.6 jit_solution(9984306392826423086)
XLA Ops:
  0.6 0.0 copy-start
  0.6 0.0 copy-start.1
  0.7 449.1 %shard_map.58 = (bf16[4,800,4096]{2,1,0:T(8,128)(2,1)}, f32[4,8,128]{2,1,0:T(8,128)}) custom-call(f32[4,6400,512]{2,1,0:T(8,128)} %w.1), custom_call_target="tpu_custom_call" | custom-call | tf_op jit(solution)/shard_map/pallas_call | solution.py:170
  449.8 0.7 slice_bitcast_fusion
  450.5 0.8 slice.7
  451.3 0.6 pad_maximum_fusion
  451.9 0.0 copy-done
  451.9 0.0 copy-done.1
  451.9 170.7 %all_gather.6 = bf16[4096,4]{0,1:T(4,128)(2,1)S(1)} all-gather(bf16[512,4]{0,1:T(4,128)(2,1)S(1)} %multiply_convert_fusion), channel_id=1, replica_groups=mesh['ep'=4,'fsdp'=8] {'fsdp'}, dimensions={0}, use_global_device_ids=true | all-gather | bytes 36864 | tf_op jit(solution)/shard_map/all_gather | solution.py:200
  622.6 5.4 all-gather
  628.0 0.7 reshape.12
  628.7 17.9 %copy.10 = bf16[4,800,4096]{2,1,0:T(8,128)(2,1)} copy(bf16[4,800,4096]{2,1,0:T(8,128)(2,1)} %get-tuple-element.10) | data formatting | bytes 52428800
  (2 shorter events, 0.0 us)
Async XLA Ops:
  0.6 451.3 %copy-start = (f32[512,4]{0,1:T(4,128)S(1)}, f32[512,4]{0,1:T(4,128)}, u32[]{:S(2)}) copy-start(f32[512,4]{0,1:T(4,128)} %param.4) | copy-start | bytes 24580
  0.6 451.3 %copy-start.1 = (f32[512]{0:T(512)S(1)}, f32[512]{0:T(512)}, u32[]{:S(2)}) copy-start(f32[512]{0:T(512)} %param.5) | copy-start | bytes 6148
